TPU v7x, 32 devices: a whole 2x2x4 slice. The times are simulated.
32 devices in a mesh: path: 8 (over y, x, core), tm: 4 (over z).
Axes of the slice: x: 2, y: 2, z: 4, core: 2. Of those that a mesh axis runs over, the one named last changes fastest.
Arguments:
- increments: bfloat16 [8192, 32, 1000], P(('path', 'tm')), may hold values from -6 to 6
- level_table: int32 [4096], replicated, may hold values from 0 to 4, as said below
- time_table: int32 [4096], replicated, may hold values from 0 to 31, as said below
Outputs:
- value_est: float32 [32], P('tm')
- grad_est: float32 [32, 1000], P('tm')
Inputs may be any that keep to these rules, and one draw needn't show every extreme that they name: `level_table`: never falls from one block to the next. `time_table`: split the 32 time points into as many runs of consecutive points as the tm axis has devices; the 128 consecutive entries of each device fall equally into every run.
All inputs are finite; a program needn't handle non-finite values.
Results may differ from a plain program's by a relative error of at most 0.0003.
The roundings to bfloat16 on the way count: a program that leaves them out, or rounds other values in their place, can miss the bound.
Values may be sent and summed in bfloat16 or wider, within the bound.
No kernel may reach another device: no remote copies, remote signals or barrier semaphores. Data moves between devices by JAX's collectives and lax.ppermute only.
A program may use at most 128 MiB of HBM per device.

v0:
```python
import jax
import jax.numpy as jnp
from jax import lax
from jax.sharding import PartitionSpec as P

LEVELS = 5
BLOCK = 2
horizon = 0.3


def stride_weights(levels, starts, steps_k, step_len):
    steps = jnp.arange(steps_k)
    fine_stride = jnp.power(2, LEVELS - 1 - levels).astype(jnp.int32)
    coarse = fine_stride * 2
    live_steps = steps[None, :] >= starts[:, None]
    on_fine = steps[None, :] % fine_stride[:, None] == 0
    on_coarse = (steps[None, :] % coarse[:, None] == 0) & (levels[:, None] > 0)
    term = fine_stride[:, None] * on_fine.astype(jnp.int32) - coarse[:, None] * on_coarse.astype(
        jnp.int32
    )
    return step_len * (live_steps.astype(jnp.float32) * term.astype(jnp.float32))


def terminal(incr, starts):
    steps_k = incr.shape[1]
    width = incr.shape[2]
    step_len = horizon / steps_k
    steps = jnp.arange(steps_k)
    live_steps = (steps[None, :] >= starts[:, None]).astype(jnp.bfloat16)
    end_point = jnp.sqrt(step_len) * jnp.einsum(
        "pi,pid->pd", live_steps, incr, preferred_element_type=jnp.float32
    )
    remaining = horizon - starts.astype(jnp.float32) * step_len
    scaled = end_point / remaining[:, None]
    end_value = 1.0 / (2.0 + 0.4 * jnp.sum(end_point * end_point, axis=1) / width)
    return (scaled, end_value)


def partial_sums(path_total, scaled, row_index, path_share, row_count):
    select = (row_index[:, None] == jnp.arange(row_count)[None, :]).astype(jnp.float32)
    select = select * (path_share * path_total)[:, None]
    return (jnp.sum(select, axis=0), jnp.dot(select.T, scaled, precision=lax.Precision.HIGHEST))


def first_terms(incr, levels, starts, path_share, row_count, offset):
    scaled, end_value = terminal(incr, starts)
    path_total = end_value * (levels == 0).astype(jnp.float32)
    return partial_sums(path_total, scaled, starts - offset, path_share, row_count)


def second_terms(incr, levels, starts, path_share, value_one, grad_low, row_count, offset):
    paths, steps_k, width = incr.shape
    step_len = horizon / steps_k
    scaled, end_value = terminal(incr, starts)
    inner_dots = jnp.dot(
        incr.reshape(paths * steps_k, width), grad_low.T, preferred_element_type=jnp.float32
    ).reshape(paths, steps_k, steps_k)
    steps = jnp.arange(steps_k)
    window = (steps[None, :, None] >= starts[:, None, None]) & (
        steps[None, :, None] < steps[None, None, :]
    )
    estimate = value_one[None, :] + jnp.sqrt(step_len) * jnp.sum(
        inner_dots * window.astype(jnp.float32), axis=1
    )
    drift_term = estimate - estimate * estimate * estimate
    weights = stride_weights(levels, starts, steps_k, step_len)
    path_total = end_value * (levels == 0).astype(jnp.float32) + jnp.sum(
        weights * drift_term, axis=1
    )
    return partial_sums(path_total, scaled, starts - offset, path_share, row_count)


def shards(increments, level_table, time_table):
    groups = lax.axis_size("tm")
    devices = lax.axis_size("path") * groups
    my_index = lax.axis_index("path") * groups + lax.axis_index("tm")
    blk_dev = level_table.shape[0] // devices
    steps_k = increments.shape[1]
    lvl_hot = (level_table[:, None] == jnp.arange(LEVELS)[None, :]).astype(jnp.float32)
    time_hot = (time_table[:, None] == jnp.arange(steps_k)[None, :]).astype(jnp.float32)
    counts = jnp.dot(lvl_hot.T, time_hot, precision=lax.Precision.HIGHEST)
    own_levels = lax.dynamic_slice_in_dim(level_table, my_index * blk_dev, blk_dev)
    own_times = lax.dynamic_slice_in_dim(time_table, my_index * blk_dev, blk_dev)
    lvl_path = jnp.repeat(own_levels, BLOCK)
    time_path = jnp.repeat(own_times, BLOCK)
    path_share = 1.0 / (BLOCK * counts[lvl_path, time_path])
    value_one, grad_one = lax.psum(
        first_terms(increments, lvl_path, time_path, path_share, steps_k, 0), ("path", "tm")
    )
    grad_low = grad_one.astype(jnp.bfloat16)
    value_part, grad_part = lax.psum_scatter(
        second_terms(increments, lvl_path, time_path, path_share, value_one, grad_low, steps_k, 0),
        "tm",
        scatter_dimension=0,
        tiled=True,
    )
    value_est, grad_est = lax.psum((value_part, grad_part), "path")
    return (value_est, grad_est)


def solution(mesh):
    placed = (P(("path", "tm"), None, None), P(), P())
    return jax.shard_map(
        shards, mesh=mesh, in_specs=placed, out_specs=(P("tm"), P("tm", None)), check_vma=False
    )
```

profile of v0, /device:TPU:0, one launch (start us, length us, event | category | flops | bytes accessed | tf_op | source)
XLA Modules:
  0.0 158.6 jit_solution(13497619476478879534)
XLA Ops:
  7.2 0.0 reduce-scatter.2.cloned.1.call-start
  7.2 0.8 broadcast_compare_fusion
  8.0 0.8 dynamic_slice.6
  8.7 0.9 fusion
  9.7 0.1 broadcast_in_dim.22
  9.8 0.2 reshape.283
  9.9 0.1 eq.74
  10.1 0.1 broadcast_in_dim.23
  10.2 0.1 reshape.282
  10.4 23.5 %copy.11 = bf16[256,32,1000]{2,1,0:T(8,128)(2,1)} copy(bf16[256,32,1000]{0,2,1:T(8,128)(2,1)} %param.5) | data formatting | bytes 32768000 | tf_op args[0]
  33.9 7.1 %multiply_reduce_fusion = f32[256,1000]{0,1:T(8,128)S(1)} fusion(bf16[256,32,1000]{0,2,1:T(8,128)(2,1)} %param.5, f32[256,32]{0,1:T(8,128)S(1)} %get-tuple-element.18), kind=kLoop, calls=%fused_computation.1 | loop fusion | flops 24320000 | bytes 17440768 | tf_op jit(solution)/shard_map/pi,pid->pd/dot_general | solution.py:30
  41.0 0.2 multiply_reduce_fusion.1
  41.1 0.1 broadcast_in_dim.24
  41.2 0.1 eq.85
  41.4 1.4 gather_fusion
  42.8 0.1 select_reduce_fusion.2
  42.9 1.0 fusion.2
  43.9 0.0 copy-start
  43.9 44.4 %all-reduce.1 = (bf16[32,1000]{1,0:T(8,128)(2,1)S(1)}, f32[32]{0:T(128)S(1)}) all-reduce(f32[32,1000]{1,0:T(8,128)S(1)} %fusion.2, f32[32]{0:T(128)S(1)} %select_reduce_fusion.2), channel_id=1, replica_groups=mesh['path'=8,'tm'=4] {'path','tm'}, use_global_device_ids=true, to_apply=%region_3.5 | all-reduce | flops 32032 | bytes 192256 | tf_op jit(solution)/shard_map/psum | solution.py:87
  88.3 10.7 %convolution_bitcast_fusion = f32[8192,32]{0,1:T(8,128)S(1)} fusion(bf16[8192,1000]{1,0:T(8,128)(2,1)} %bitcast.11, bf16[32,1000]{1,0:T(8,128)(2,1)S(1)} %get-tuple-element.3), kind=kOutput, calls=%fused_computation.2 | convolution fusion | flops 524288000 | bytes 17496576 | tf_op jit(solution)/shard_map/dot_general | solution.py:55
  99.0 2.7 %reshape.285 = f32[256,32,32]{1,0,2:T(8,128)} reshape(f32[8192,32]{0,1:T(8,128)S(1)} %convolution_bitcast_fusion) | data formatting | bytes 2097152 | tf_op jit(solution)/shard_map/reshape | solution.py:57
  101.7 0.1 copy.10
  101.9 0.1 broadcast.622
  102.0 0.1 reshape.301
  102.1 0.1 broadcast.629
  102.2 0.1 reshape.303
  102.4 0.1 broadcast_in_dim.28
  102.5 0.1 ne.146
  102.6 0.1 broadcast.601
  102.7 0.1 reshape.291
  102.8 0.1 broadcast.611
  102.9 0.1 reshape.297
  103.1 0.1 broadcast_in_dim.29
  103.2 0.2 select_n.157
  103.3 0.1 broadcast_in_dim.30
  103.4 0.1 gt.14
  103.6 3.3 %select_reduce_fusion = f32[256,32]{0,1:T(8,128)S(1)} fusion(f32[256,32,32]{1,0,2:T(8,128)} %reshape.285, pred[32,32]{0,1:T(8,128)(4,1)S(1)} %iota_compare_fusion.8, pred[256,32]{1,0:T(8,128)(4,1)S(1)} %copy.10), kind=kLoop, calls=%fused_computation.3 | loop fusion | flops 778240 | bytes 1090560 | tf_op jit(solution)/shard_map/reduce_sum | solution.py:62
  106.9 0.7 fusion.9
  107.6 1.6 %fusion.1 = f32[32,1000]{1,0:T(8,128)} fusion(f32[256,1000]{0,1:T(8,128)S(1)} %multiply_reduce_fusion, f32[256]{0:T(256)S(1)} %get-tuple-element.26, f32[256]{0:T(256)S(1)} %add_multiply_fusion, s32[256]{0:T(256)S(1)} %eq.74), kind=kOutput, calls=%fused_computation.8 | convolution fusion | flops 98832384 | bytes 1155072 | tf_op jit(solution)/shard_map/dot_general | solution.py:42
  109.3 0.0 reduce-scatter.2.cloned.1.call-update
  109.3 0.0 copy-done
  109.3 0.6 dynamic-slice
  110.5 0.1 select_reduce_fusion.1
  110.7 10.6 %all-reduce = f32[32]{0:T(128)S(1)} all-reduce(f32[32]{0:T(128)S(1)} %select_reduce_fusion.1), channel_id=2, replica_groups=mesh['path'=8,'tm'=4] {'tm'}, use_global_device_ids=true, to_apply=%region_7.9.clone | all-reduce | flops 32 | bytes 256
  121.2 0.1 dynamic-slice.1
  121.3 6.6 %reduce-scatter.2.cloned.1.call-done = f32[8,1000]{1,0:T(8,128)} async-done(((f32[32,1000]{1,0:T(8,128)}), f32[8,1000]{1,0:T(8,128)}) %reduce-scatter.2.cloned.1.call-update) | async-done | bytes 32016 | tf_op jit(solution)/shard_map/reduce_scatter | solution.py:91
  127.9 23.9 %all-reduce.2 = (f32[8]{0:T(128)}, f32[8,1000]{1,0:T(8,128)}) all-reduce(f32[8]{0:T(128)S(1)} %dynamic-slice.1, f32[8,1000]{1,0:T(8,128)} %reduce-scatter.2.cloned.1.call-done), channel_id=1, replica_groups=mesh['path'=8,'tm'=4] {'path'}, use_global_device_ids=true, to_apply=%region_8.10 | all-reduce | flops 8008 | bytes 64064 | tf_op jit(solution)/shard_map/psum | solution.py:97
  (12 shorter events, 0.2 us)
Async XLA Ops:
  7.2 120.7 %reduce-scatter.2.cloned.1.call-start = ((), (), s32[]{:S(2)}) async-start(), calls=%async_computation.1 | async-start | bytes 163840 | tf_op jit(solution)/shard_map/reduce_scatter | solution.py:91
  43.9 65.4 %copy-start = (u32[32]{0:T(128)S(1)}, u32[32]{0:T(128)}, u32[]{:S(2)}) copy-start(u32[32]{0:T(128)} %constant.92) | copy-start | bytes 388
Sparse Core Ops, SparseCore 0:
  109.4 18.4 reduce-scatter.1
where the time goes:
time: 160 us; the launch traced here: 159 us
  blocking collectives  78.9 us (49%)
  local copies, waits for them, and re-layouts  31.6 us (20%)
  between operations  14.9 us (9%)
  matrix products  14.2 us (9%)
  other arithmetic  12.4 us (8%)
  waiting for transfers between devices  6.62 us (4%)
    psum x1, blocking collectives, shards(): lax.psum(first_terms(increments, lvl_path, time_path, path_share, steps_k...  44.4 us
    unnamed x5, local copies, waits for them, and re-layouts  24.1 us
    psum x1, blocking collectives, shards(): value_est, grad_est = lax.psum((value_part, grad_part), 'path')  23.9 us
    dot_general x1, matrix products, second_terms(): jnp.dot(incr.reshape(paths * steps_k, width), grad_low.T, preferred_eleme...  10.7 us
    unnamed x1, blocking collectives  10.6 us
    dot_general x1, other arithmetic, terminal(): jnp.einsum('pi,pid->pd', live_steps, incr, preferred_element_type=jnp.flo...  7.07 us
    reduce_scatter x1, waiting for transfers between devices, shards(): lax.psum_scatter(second_terms(increments, lvl_path, time_path, path_share...  6.6 us
    reduce_sum x1, other arithmetic, second_terms(): jnp.sum(inner_dots * window.astype(jnp.float32), axis=1)  3.35 us
  transfers between devices with their start and end apart: 1, of which 1 were waited for; matrix products, arithmetic and copies ran while one was open for 0% of the time, Pallas kernels for 0%

commit v1 on v0

--- a/solution.py
+++ b/solution.py
@@ -6,6 +6,10 @@
 LEVELS = 5
 BLOCK = 2
 horizon = 0.3
+
+
+def bring_shapes_in(panel):
+    return lax.psum(lax.psum(panel, "path"), "tm")
 
 
 def stride_weights(levels, starts, steps_k, step_len):
@@ -84,8 +88,8 @@
     lvl_path = jnp.repeat(own_levels, BLOCK)
     time_path = jnp.repeat(own_times, BLOCK)
     path_share = 1.0 / (BLOCK * counts[lvl_path, time_path])
-    value_one, grad_one = lax.psum(
-        first_terms(increments, lvl_path, time_path, path_share, steps_k, 0), ("path", "tm")
+    value_one, grad_one = bring_shapes_in(
+        first_terms(increments, lvl_path, time_path, path_share, steps_k, 0)
     )
     grad_low = grad_one.astype(jnp.bfloat16)
     value_part, grad_part = lax.psum_scatter(

time: 160 us -> 166 us (1.038)
  waiting for transfers between devices: 6.62 us -> 22.3 us
  blocking collectives: 78.9 us -> 69.2 us
    psum x0 -> x1, waiting for transfers between devices: none -> 15.6 us  [bring_shapes_in(): return lax.psum(lax.psum(panel, 'path'), 'tm')]
    psum x1 -> x2, blocking collectives: 44.4 us -> 36.9 us  [bring_shapes_in(): return lax.psum(lax.psum(panel, 'path'), 'tm')]
    unnamed x1, blocking collectives: 10.6 us -> 8.37 us
  transfers between devices with their start and end apart: 1 -> 2, of which waited for: 1 -> 2; matrix products, arithmetic and copies ran while one was open for 0% -> 16% of each run, Pallas kernels for 0% -> 0%
where the time goes in v1:
time: 166 us; the launch traced here: 165 us
  blocking collectives  69.2 us (42%)
  local copies, waits for them, and re-layouts  31.6 us (19%)
  waiting for transfers between devices  22.3 us (13%)
  matrix products  14.9 us (9%)
  between operations  14.9 us (9%)
  other arithmetic  12.4 us (7%)
    psum x2, blocking collectives, bring_shapes_in(): return lax.psum(lax.psum(panel, 'path'), 'tm')  36.9 us
    unnamed x5, local copies, waits for them, and re-layouts  24.1 us
    psum x1, blocking collectives, shards(): value_est, grad_est = lax.psum((value_part, grad_part), 'path')  23.9 us
    psum x1, waiting for transfers between devices, bring_shapes_in(): return lax.psum(lax.psum(panel, 'path'), 'tm')  15.6 us
    dot_general x1, matrix products, second_terms(): jnp.dot(incr.reshape(paths * steps_k, width), grad_low.T, preferred_eleme...  10.7 us
    unnamed x1, blocking collectives  8.37 us
    dot_general x1, other arithmetic, terminal(): jnp.einsum('pi,pid->pd', live_steps, incr, preferred_element_type=jnp.flo...  7.07 us
    reduce_scatter x1, waiting for transfers between devices, shards(): lax.psum_scatter(second_terms(increments, lvl_path, time_path, path_share...  6.65 us
  transfers between devices with their start and end apart: 2, of which 2 were waited for; matrix products, arithmetic and copies ran while one was open for 16% of the time, Pallas kernels for 0%

profile of v1, /device:TPU:0, one launch (start us, length us, event | category | flops | bytes accessed | tf_op | source)
XLA Modules:
  0.0 165.3 jit_solution(1685073692375863786)
XLA Ops:
  7.2 0.0 all-reduce.5.cloned.1.call-start
  7.2 0.8 broadcast_compare_fusion
  8.0 0.8 dynamic_slice.6
  8.7 0.9 fusion
  9.7 0.1 broadcast_in_dim.22
  9.8 0.2 reshape.283
  9.9 0.1 eq.74
  10.1 0.1 broadcast_in_dim.23
  10.2 0.1 reshape.282
  10.3 7.1 %multiply_reduce_fusion = f32[256,1000]{0,1:T(8,128)S(1)} fusion(bf16[256,32,1000]{0,2,1:T(8,128)(2,1)} %param.5, f32[256,32]{0,1:T(8,128)S(1)} %get-tuple-element.18), kind=kLoop, calls=%fused_computation.1 | loop fusion | flops 24320000 | bytes 17440768 | tf_op jit(solution)/shard_map/pi,pid->pd/dot_general | solution.py:34
  17.4 0.2 multiply_reduce_fusion.1
  17.6 0.1 broadcast_in_dim.24
  17.7 0.1 eq.85
  17.8 1.4 gather_fusion
  19.3 1.6 fusion.2
  20.9 0.0 all-reduce.5.cloned.1.call-update
  20.9 0.0 reduce-scatter.2.cloned.1.call-start
  21.0 0.1 select_reduce_fusion.2
  21.1 23.5 %copy.11 = bf16[256,32,1000]{2,1,0:T(8,128)(2,1)} copy(bf16[256,32,1000]{0,2,1:T(8,128)(2,1)} %param.5) | data formatting | bytes 32768000 | tf_op args[0]
  44.6 0.0 copy-start
  44.7 15.2 %psum.42 = f32[32]{0:T(128)S(1)} all-reduce(f32[32]{0:T(128)S(1)} %select_reduce_fusion.2), channel_id=1, replica_groups=mesh['path'=8,'tm'=4] {'path'}, use_global_device_ids=true, to_apply=%region_2.4 | all-reduce | flops 32 | bytes 256 | tf_op jit(solution)/shard_map/psum | solution.py:12
  59.8 0.1 copy.10
  60.0 0.1 broadcast.622
  60.1 0.2 reshape.301
  60.2 0.1 broadcast.629
  60.3 0.1 reshape.303
  60.4 0.1 broadcast_in_dim.28
  60.5 0.1 ne.146
  60.7 0.1 broadcast.601
  60.8 0.1 reshape.291
  60.9 0.1 broadcast.611
  61.0 0.1 reshape.297
  61.2 0.1 broadcast_in_dim.29
  61.3 0.2 select_n.157
  61.4 0.1 broadcast_in_dim.30
  61.5 0.1 gt.14
  61.7 15.6 %all-reduce.5.cloned.1.call-done = f32[32,1000]{1,0:T(8,128)} async-done(((f32[32,1000]{1,0:T(8,128)}), f32[32,1000]{1,0:T(8,128)}) %all-reduce.5.cloned.1.call-update) | async-done | bytes 128016 | tf_op jit(solution)/shard_map/psum | solution.py:12
  77.3 21.8 %all-reduce.2 = (bf16[32,1000]{1,0:T(8,128)(2,1)S(1)}, f32[32]{0:T(128)S(1)}) all-reduce(f32[32,1000]{1,0:T(8,128)} %all-reduce.5.cloned.1.call-done, f32[32]{0:T(128)S(1)} %psum.42), channel_id=1, replica_groups=mesh['path'=8,'tm'=4] {'tm'}, use_global_device_ids=true, to_apply=%region_5.7 | all-reduce | flops 32032 | bytes 192256 | tf_op jit(solution)/shard_map/psum | solution.py:12
  99.1 10.7 %convolution_bitcast_fusion = f32[8192,32]{0,1:T(8,128)S(1)} fusion(bf16[8192,1000]{1,0:T(8,128)(2,1)} %bitcast.11, bf16[32,1000]{1,0:T(8,128)(2,1)S(1)} %get-tuple-element.5), kind=kOutput, calls=%fused_computation.2 | convolution fusion | flops 524288000 | bytes 17496576 | tf_op jit(solution)/shard_map/dot_general | solution.py:59
  109.8 2.7 %reshape.285 = f32[256,32,32]{1,0,2:T(8,128)} reshape(f32[8192,32]{0,1:T(8,128)S(1)} %convolution_bitcast_fusion) | data formatting | bytes 2097152 | tf_op jit(solution)/shard_map/reshape | solution.py:61
  112.5 3.3 %select_reduce_fusion = f32[256,32]{0,1:T(8,128)S(1)} fusion(f32[256,32,32]{1,0,2:T(8,128)} %reshape.285, pred[32,32]{0,1:T(8,128)(4,1)S(1)} %iota_compare_fusion.8, pred[256,32]{1,0:T(8,128)(4,1)S(1)} %copy.10), kind=kLoop, calls=%fused_computation.3 | loop fusion | flops 778240 | bytes 1090560 | tf_op jit(solution)/shard_map/reduce_sum | solution.py:66
  115.8 0.7 fusion.9
  116.5 1.6 fusion.1
  118.1 0.0 reduce-scatter.2.cloned.1.call-update
  118.2 0.0 copy-done
  118.2 0.6 dynamic-slice
  119.4 0.1 select_reduce_fusion.1
  119.5 8.4 %all-reduce = f32[32]{0:T(128)S(1)} all-reduce(f32[32]{0:T(128)S(1)} %select_reduce_fusion.1), channel_id=2, replica_groups=mesh['path'=8,'tm'=4] {'tm'}, use_global_device_ids=true, to_apply=%region_9.11.clone | all-reduce | flops 32 | bytes 256
  127.9 0.1 dynamic-slice.1
  128.0 6.7 %reduce-scatter.2.cloned.1.call-done = f32[8,1000]{1,0:T(8,128)} async-done(((f32[32,1000]{1,0:T(8,128)}), f32[8,1000]{1,0:T(8,128)}) %reduce-scatter.2.cloned.1.call-update) | async-done | bytes 32016 | tf_op jit(solution)/shard_map/reduce_scatter | solution.py:95
  134.6 23.9 %all-reduce.1 = (f32[8]{0:T(128)}, f32[8,1000]{1,0:T(8,128)}) all-reduce(f32[8]{0:T(128)S(1)} %dynamic-slice.1, f32[8,1000]{1,0:T(8,128)} %reduce-scatter.2.cloned.1.call-done), channel_id=1, replica_groups=mesh['path'=8,'tm'=4] {'path'}, use_global_device_ids=true, to_apply=%region_10.12 | all-reduce | flops 8008 | bytes 64064 | tf_op jit(solution)/shard_map/psum | solution.py:101
  (13 shorter events, 0.2 us)
Async XLA Ops:
  7.2 70.1 %all-reduce.5.cloned.1.call-start = ((), (), s32[]{:S(2)}) async-start(), calls=%async_computation.1 | async-start | bytes 262144 | tf_op jit(solution)/shard_map/psum | solution.py:12
  20.9 113.7 %reduce-scatter.2.cloned.1.call-start = ((), (), s32[]{:S(2)}) async-start(), calls=%async_computation.2 | async-start | bytes 163840 | tf_op jit(solution)/shard_map/reduce_scatter | solution.py:95
  44.6 73.6 %copy-start = (u32[32]{0:T(128)S(1)}, u32[32]{0:T(128)}, u32[]{:S(2)}) copy-start(u32[32]{0:T(128)} %constant.92) | copy-start | bytes 388
Sparse Core Ops, SparseCore 0:
  21.1 56.1 all-reduce.4
  118.3 16.2 reduce-scatter.1
